TPU v7x, 32 devices: a whole 2x2x4 slice. The times are simulated.
32 devices in a mesh: heads: 2 (over x), seq: 16 (over z, y, core).
Axes of the slice: x: 2, y: 2, z: 4, core: 2. Of those that a mesh axis runs over, the one named last changes fastest.
Arguments:
- q_nope: bfloat16 [1152, 64, 128], P('seq', 'heads'), may hold values from -6 to 6
- q_rope: bfloat16 [1152, 64, 64], P('seq', 'heads'), may hold values from -125 to 125
- latent: bfloat16 [1152, 512], P('seq'), may hold values from -6 to 6
- key_rope: bfloat16 [1152, 64], P('seq'), may hold values from -5 to 5
- absorb_key: bfloat16 [64, 128, 512], P('heads'), may hold values from -0.5 to 0.5
- absorb_value: bfloat16 [64, 512, 128], P('heads'), may hold values from -0.25 to 0.25
- w_out: bfloat16 [8192, 3584], P('heads', 'seq'), may hold values from -0.125 to 0.125
- residual: bfloat16 [1152, 3584], P(('seq', 'heads')), may hold values from -2 to 2
- norm_gain: float32 [3584], replicated, may hold values from 0.25 to 1.75
- span_table: int32 [32], replicated, may hold values from 0 to 31, each once
Outputs:
- new_residual: bfloat16 [1152, 3584], P(('seq', 'heads'))
- normed: bfloat16 [1152, 3584], P(('seq', 'heads'))
Inputs may be any that keep to these rules, and one draw needn't show every extreme that they name: `span_table`: A permutation of the span numbers.
All inputs are finite; a program needn't handle non-finite values.
Results may differ from a plain program's by a relative error of at most 0.014.
Values may be sent and summed in bfloat16 or wider, within the bound.
No kernel may reach another device: no remote copies, remote signals or barrier semaphores. Data moves between devices by JAX's collectives and lax.ppermute only.
A program may use at most 128 MiB of HBM per device.

v0:
```python
import jax
import jax.numpy as jnp
from jax import lax
from jax.sharding import PartitionSpec as P

score_scale = 192.0 ** (-0.5)


def place_rows(start, count, span_len, span_table):
    index = start + jnp.arange(count, dtype=jnp.int32)
    which = index // span_len
    picked = jnp.where(
        which[:, None] == jnp.arange(span_table.shape[0], dtype=jnp.int32)[None, :],
        span_table[None, :],
        0,
    )
    return jnp.sum(picked, axis=1) * span_len + index % span_len


def per_device(
    q_nope,
    q_rope,
    latent,
    key_rope,
    absorb_key,
    absorb_value,
    w_out,
    residual,
    norm_gain,
    span_table,
):
    tok_rows = q_nope.shape[0]
    span_len = tok_rows // 2
    seq_count = lax.axis_size("seq")
    my_start = lax.axis_index("seq") * tok_rows
    query_pos = place_rows(my_start, tok_rows, span_len, span_table)
    q_lat = jnp.einsum(
        "thd,hdl->htl", q_nope, absorb_key, preferred_element_type=jnp.float32
    ).astype(jnp.bfloat16)
    rotary = jnp.transpose(q_rope, (1, 0, 2))
    local_heads = q_lat.shape[0]

    def attend(carry, pieces, start):
        top, total, summed = carry
        lat_piece, rope_piece = pieces
        key_pos = place_rows(start, lat_piece.shape[0], span_len, span_table)
        score = jnp.einsum("htl,nl->htn", q_lat, lat_piece, preferred_element_type=jnp.float32)
        score = (
            score
            + jnp.einsum("htr,nr->htn", rotary, rope_piece, preferred_element_type=jnp.float32)
        ) * score_scale
        seen = (key_pos[None, :] <= query_pos[:, None])[None, :, :]
        score = jnp.where(seen, score, jnp.float32(-1e30))
        fresh = jnp.maximum(top, jnp.max(score, axis=2))
        weight = jnp.where(seen, jnp.exp(score - fresh[:, :, None]), jnp.float32(0.0))
        factor = jnp.exp(top - fresh)
        total = total * factor + jnp.sum(weight, axis=2)
        summed = summed * factor[:, :, None] + jnp.einsum(
            "htn,nl->htl",
            weight.astype(jnp.bfloat16),
            lat_piece,
            preferred_element_type=jnp.float32,
        )
        return (fresh, total, summed)

    start_carry = (
        jnp.full((local_heads, tok_rows), -1e30, jnp.float32),
        jnp.zeros((local_heads, tok_rows), jnp.float32),
        jnp.zeros((local_heads, tok_rows, latent.shape[1]), jnp.float32),
    )
    all_lat, all_rope = (
        lax.all_gather(latent, "seq", axis=0, tiled=True),
        lax.all_gather(key_rope, "seq", axis=0, tiled=True),
    )
    block = tok_rows * min(8, seq_count)
    steps_count = all_lat.shape[0] // block

    def visit(step, carry):
        begin = (step * block).astype(jnp.int32)
        lat_piece = lax.dynamic_slice_in_dim(all_lat, begin, block, 0)
        rope_piece = lax.dynamic_slice_in_dim(all_rope, begin, block, 0)
        return attend(carry, (lat_piece, rope_piece), begin)

    top, total, summed = lax.fori_loop(0, steps_count, visit, start_carry)
    context = (summed / total[:, :, None]).astype(jnp.bfloat16)
    per_head = jnp.einsum(
        "htl,hle->the", context, absorb_value, preferred_element_type=jnp.float32
    ).astype(jnp.bfloat16)
    heads_out = per_head.reshape(tok_rows, local_heads * per_head.shape[2])
    every_row = lax.all_gather(heads_out, "seq", axis=0, tiled=True)
    columns = jnp.dot(every_row, w_out, preferred_element_type=jnp.float32).astype(jnp.bfloat16)
    partial_value = lax.all_to_all(columns, "seq", split_axis=0, concat_axis=1, tiled=True).astype(
        jnp.float32
    )
    projected = lax.psum_scatter(
        partial_value.astype(jnp.bfloat16), "heads", scatter_dimension=0, tiled=True
    ).astype(jnp.float32)
    hidden = residual.astype(jnp.float32) + projected
    new_residual = hidden.astype(jnp.bfloat16)
    scale = lax.rsqrt(jnp.mean(hidden * hidden, axis=1, keepdims=True) + 1e-06)
    normed = (hidden * scale * norm_gain[None, :]).astype(jnp.bfloat16)
    return (new_residual, normed)


def solution(mesh):
    in_specs = (
        P("seq", "heads", None),
        P("seq", "heads", None),
        P("seq", None),
        P("seq", None),
        P("heads", None, None),
        P("heads", None, None),
        P("heads", "seq"),
        P(("seq", "heads"), None),
        P(),
        P(),
    )
    out_specs = (P(("seq", "heads"), None), P(("seq", "heads"), None))
    return jax.shard_map(
        per_device, mesh=mesh, in_specs=in_specs, out_specs=out_specs, check_vma=False
    )
```

profile of v0, /device:TPU:0, one launch (start us, length us, event | category | flops | bytes accessed | tf_op | source)
XLA Modules:
  0.0 225.6 jit_solution(14816708200302043049)
XLA Ops:
  7.2 0.7 all-gather.4.cloned.1.call-update
  8.0 24.1 %all-gather = bf16[16,72,64]{1,2,0:T(8,128)(2,1)S(1)} all-gather(bf16[1,72,64]{1,2,0:T(8,128)(2,1)} %bitcast.47), channel_id=1, replica_groups=mesh['heads'=2,'seq'=16] {'seq'}, dimensions={0}, use_global_device_ids=true | all-gather | bytes 156672 | tf_op jit(solution)/shard_map/all_gather | solution.py:73
  32.6 0.7 select_reduce_fusion.1
  33.4 4.7 %convolution_convert_fusion.1 = bf16[32,72,512]{2,1,0:T(8,128)(2,1)} fusion(bf16[32,128,512]{2,1,0:T(8,128)(2,1)} %param.16, bf16[72,32,128]{2,1,0:T(8,128)(2,1)} %param.12), kind=kOutput, calls=%fused_computation.41 | convolution fusion | flops 303169536 | bytes 7143424 | tf_op jit(solution)/shard_map/thd,hdl->htl/dot_general | solution.py:37
  38.0 13.4 %all-gather.4.cloned.1.call-done = bf16[1152,512]{1,0:T(8,128)(2,1)} async-done(((bf16[72,512]{1,0:T(8,128)(2,1)}), bf16[1152,512]{1,0:T(8,128)(2,1)}) %all-gather.4.cloned.1.call-update) | async-done | bytes 1179664 | tf_op jit(solution)/shard_map/all_gather | solution.py:72
  51.4 36.1 %while.20 = (s32[]{:T(128)}, f32[32,72]{1,0:T(8,128)S(1)}, f32[32,72]{1,0:T(8,128)S(1)}, f32[32,72,512]{2,1,0:T(8,128)}, s32[32]{0:T(128)S(1)}, /*index=5*/s32[7...) while((s32[]{:T(128)}, f32[32,72]{1,0:T(8,128)S(1)}, ...), condition=%wide.region_5.6_spmd.clone, body=%wide.region_1.5_spmd.clone.sunk | while | flops 2904706304 | bytes 68787400 | solution.py:84
  51.4 3.9 %fusion.59 = f32[576,32,72]{0,2,1:T(8,128)S(1)} fusion(bf16[32,72,512]{2,1,0:T(8,128)(2,1)} %get-tuple-element.413, bf16[1152,512]{1,0:T(8,128)(2,1)} %get-tuple-element.412, s32[]{:T(128)S(6)} %select_n.141), kind=kOutput, calls=%fused_computation.11.clone.1 | convolution fusion | flops 1358954496 | bytes 8257540 | tf_op jit(solution)/shard_map/while/body/eval_jaxpr/htl,nl->htn/dot_general | solution.py:47
  55.6 4.2 %fusion.61 = (f32[32,72]{1,0:T(8,128)S(1)}, f32[32,72,576]{2,1,0:T(8,128)}) fusion(f32[576,32,72]{0,2,1:T(8,128)S(1)} %fusion.59, bf16[32,72,64]{1,2,0:T(8,128)(2,1)S(1)} %copy-done.3, bf16[1152,64]{0,1:T(8,128)(2,1)S(1)} %get-tuple-element.414, s32[]{:T(128)S(6)} %select_n.141, pred[72,576]{1,0:T(8,128)(4,1)S(1)} %broadcast_compare_fusion.2), kind=kOutput, calls=%fused_computation.58.clone.1 | convolution fusion | flops 175175424 | bytes 11868164 | tf_op jit(solution)/shard_map/while/body/eval_jaxpr/htr,nr->htn/dot_general | solution.py:50
  59.9 4.1 %fusion.62 = f32[32,72]{1,0:T(8,128)S(1)} fusion(f32[32,72,576]{2,1,0:T(8,128)} %get-tuple-element.375, f32[32,72]{1,0:T(8,128)S(1)} %select_maximum_fusion.2, pred[72,576]{1,0:T(8,128)(4,1)S(1)} %broadcast_compare_fusion.2), kind=kLoop, calls=%fused_computation.3.clone.1 | loop fusion | flops 3979008 | bytes 5368320 | tf_op jit(solution)/shard_map/while/body/eval_jaxpr/reduce_sum | solution.py:57
  64.3 4.4 %fusion.64 = f32[32,72,512]{2,1,0:T(8,128)} fusion(f32[32,72,512]{2,1,0:T(8,128)} %get-tuple-element.395, f32[32,72]{1,0:T(8,128)S(1)} %get-tuple-element.377, pred[]{:T(512)S(6)} %compare.3, f32[32,72,576]{2,1,0:T(8,128)S(1)} %copy-done.1, f32[32,72]{1,0:T(8,128)S(1)} %select_maximum_fusion.2, pred[72,576]{1,0:T(8,128)(4,1)S(1)} %broadcast_compare_fusion.2, ...), kind=kOutput, calls=%fused_computation.5.clone.1 | convolution fusion | flops 1366474752 | bytes 16004101 | tf_op jit(solution)/shard_map/while/body/eval_jaxpr/htn,nl->htl/dot_general | solution.py:58
  68.6 3.9 %fusion.59 = f32[576,32,72]{0,2,1:T(8,128)S(1)} fusion(bf16[32,72,512]{2,1,0:T(8,128)(2,1)} %get-tuple-element.413, bf16[1152,512]{1,0:T(8,128)(2,1)} %get-tuple-element.412, s32[]{:T(128)S(6)} %select_n.141), kind=kOutput, calls=%fused_computation.11.clone.1 | convolution fusion | flops 1358954496 | bytes 8257540 | tf_op jit(solution)/shard_map/while/body/eval_jaxpr/htl,nl->htn/dot_general | solution.py:47
  72.8 4.2 %fusion.61 = (f32[32,72]{1,0:T(8,128)S(1)}, f32[32,72,576]{2,1,0:T(8,128)}) fusion(f32[576,32,72]{0,2,1:T(8,128)S(1)} %fusion.59, bf16[32,72,64]{1,2,0:T(8,128)(2,1)S(1)} %copy-done.3, bf16[1152,64]{0,1:T(8,128)(2,1)S(1)} %get-tuple-element.414, s32[]{:T(128)S(6)} %select_n.141, pred[72,576]{1,0:T(8,128)(4,1)S(1)} %broadcast_compare_fusion.2), kind=kOutput, calls=%fused_computation.58.clone.1 | convolution fusion | flops 175175424 | bytes 11868164 | tf_op jit(solution)/shard_map/while/body/eval_jaxpr/htr,nr->htn/dot_general | solution.py:50
  77.1 4.1 %fusion.62 = f32[32,72]{1,0:T(8,128)S(1)} fusion(f32[32,72,576]{2,1,0:T(8,128)} %get-tuple-element.375, f32[32,72]{1,0:T(8,128)S(1)} %select_maximum_fusion.2, pred[72,576]{1,0:T(8,128)(4,1)S(1)} %broadcast_compare_fusion.2), kind=kLoop, calls=%fused_computation.3.clone.1 | loop fusion | flops 3979008 | bytes 5368320 | tf_op jit(solution)/shard_map/while/body/eval_jaxpr/reduce_sum | solution.py:57
  81.5 6.0 %fusion.64 = f32[32,72,512]{2,1,0:T(8,128)} fusion(f32[32,72,512]{2,1,0:T(8,128)} %get-tuple-element.395, f32[32,72]{1,0:T(8,128)S(1)} %get-tuple-element.377, pred[]{:T(512)S(6)} %compare.3, f32[32,72,576]{2,1,0:T(8,128)S(1)} %copy-done.1, f32[32,72]{1,0:T(8,128)S(1)} %select_maximum_fusion.2, pred[72,576]{1,0:T(8,128)(4,1)S(1)} %broadcast_compare_fusion.2, ...), kind=kOutput, calls=%fused_computation.5.clone.1 | convolution fusion | flops 1366474752 | bytes 16004101 | tf_op jit(solution)/shard_map/while/body/eval_jaxpr/htn,nl->htl/dot_general | solution.py:58
  87.5 4.6 %fusion.31 = bf16[32,9,8,128]{3,2,1,0:T(8,128)(2,1)S(1)} fusion(bf16[32,512,128]{2,1,0:T(8,128)(2,1)} %param.17, f32[32,72,512]{2,1,0:T(8,128)} %get-tuple-element.248, f32[32,72]{1,0:T(8,128)S(1)} %get-tuple-element.249), kind=kOutput, calls=%fused_computation.43 | convolution fusion | flops 304644096 | bytes 9511936 | tf_op jit(solution)/shard_map/htl,hle->the/dot_general | solution.py:86
  92.1 0.9 copy.42
  93.1 79.9 %all-gather.6.cloned.1.call-done = bf16[1152,4096]{1,0:T(8,128)(2,1)} async-done(((bf16[72,4096]{1,0:T(8,128)(2,1)}), bf16[1152,4096]{1,0:T(8,128)(2,1)}) %all-gather.6.cloned.1.call-update) | async-done | bytes 9437200 | tf_op jit(solution)/shard_map/all_gather | solution.py:90
  173.0 6.7 %convolution_convert_fusion = bf16[1152,224]{0,1:T(8,128)(2,1)S(1)} fusion(bf16[1152,4096]{1,0:T(8,128)(2,1)} %all-gather.6.cloned.1.call-done, bf16[4096,224]{0,1:T(8,128)(2,1)S(1)} %copy-done), kind=kOutput, calls=%fused_computation.39 | convolution fusion | flops 2114187264 | bytes 11788288 | tf_op jit(solution)/shard_map/dot_general | solution.py:91
  180.0 20.2 %all_to_all.19 = bf16[16,72,224]{2,1,0:T(8,128)(2,1)S(1)} all-to-all(bf16[16,72,224]{2,1,0:T(8,128)(2,1)S(1)} %bitcast.45), channel_id=1, replica_groups=mesh['heads'=2,'seq'=16] {'seq'}, dimensions={0} | all-to-all | bytes 1032192 | tf_op jit(solution)/shard_map/all_to_all | solution.py:92
  200.3 1.0 all_to_all.17
  201.3 11.8 %fusion = bf16[40,3584]{1,0:T(8,128)(2,1)S(1)} fusion(bf16[72,3584]{1,0:T(8,128)(2,1)S(1)} %all_to_all.17), kind=kCustom, calls=%all-reduce-scatter | all-reduce-scatter fusion | flops 286721 | bytes 803328
  213.1 2.5 %collective-permute-start = (bf16[4,3584]{1,0:T(4,128)(2,1)S(1)}, bf16[4,3584]{1,0:T(4,128)(2,1)S(1)}, u32[]{:S(2)}, u32[]{:S(2)}) collective-permute-start(bf16[4,3584]{1,0:T(4,128)(2,1)S(1)} %slice), channel_id=1, source_target_pairs={{0,16},{1,17},{2,18},{3,19},{4,20},{5,21},{6,22},{7,23},{8,24},{9,... | collective-permute-start | bytes 86024
  215.6 0.6 dynamic-slice.4
  217.8 1.0 multiply_convert_fusion
  (53 shorter events, 3.0 us)
Async XLA Ops:
  7.2 165.8 %copy-start = (bf16[4096,224]{0,1:T(8,128)(2,1)S(1)}, bf16[4096,224]{0,1:T(8,128)(2,1)}, u32[]{:S(2)}) copy-start(bf16[4096,224]{0,1:T(8,128)(2,1)} %param.18) | copy-start | bytes 5505028
  7.2 44.2 %copy-start.6 = (s32[32]{0:T(128)S(1)}, s32[32]{0:T(128)}, u32[]{:S(2)}) copy-start(s32[32]{0:T(128)} %param.21) | copy-start | bytes 388
  7.2 44.2 %all-gather.4.cloned.1.call-start = ((), (), s32[]{:S(2)}) async-start(), calls=%async_computation.1 | async-start | bytes 1253376 | tf_op jit(solution)/shard_map/all_gather | solution.py:72
  7.9 165.1 %all-gather.6.cloned.1.call-start = ((), (), s32[]{:S(2)}) async-start(), calls=%async_computation.2 | async-start | bytes 10027008 | tf_op jit(solution)/shard_map/all_gather | solution.py:90
  51.4 4.2 %copy-start.3 = (bf16[32,72,64]{1,2,0:T(8,128)(2,1)S(1)}, bf16[32,72,64]{1,2,0:T(8,128)(2,1)}, u32[]{:S(2)}) copy-start(bf16[32,72,64]{1,2,0:T(8,128)(2,1)} %get-tuple-element.415) | copy-start | bytes 884740 | tf_op jit(solution)/shard_map/while
  55.6 8.4 %copy-start.2 = (bf16[1152,512]{1,0:T(8,128)(2,1)S(1)}, bf16[1152,512]{1,0:T(8,128)(2,1)}, u32[]{:S(2)}) copy-start(bf16[1152,512]{1,0:T(8,128)(2,1)} %get-tuple-element.412) | copy-start | bytes 3538948 | tf_op jit(solution)/shard_map/while
  59.8 4.4 %copy-start.1 = (f32[32,72,576]{2,1,0:T(8,128)S(1)}, f32[32,72,576]{2,1,0:T(8,128)}, u32[]{:S(2)}) copy-start(f32[32,72,576]{2,1,0:T(8,128)} %get-tuple-element.375) | copy-start | bytes 15925252 | tf_op jit(solution)/shard_map/while
  68.6 4.2 %copy-start.3 = (bf16[32,72,64]{1,2,0:T(8,128)(2,1)S(1)}, bf16[32,72,64]{1,2,0:T(8,128)(2,1)}, u32[]{:S(2)}) copy-start(bf16[32,72,64]{1,2,0:T(8,128)(2,1)} %get-tuple-element.415) | copy-start | bytes 884740 | tf_op jit(solution)/shard_map/while
  72.8 8.4 %copy-start.2 = (bf16[1152,512]{1,0:T(8,128)(2,1)S(1)}, bf16[1152,512]{1,0:T(8,128)(2,1)}, u32[]{:S(2)}) copy-start(bf16[1152,512]{1,0:T(8,128)(2,1)} %get-tuple-element.412) | copy-start | bytes 3538948 | tf_op jit(solution)/shard_map/while
  77.1 4.4 %copy-start.1 = (f32[32,72,576]{2,1,0:T(8,128)S(1)}, f32[32,72,576]{2,1,0:T(8,128)}, u32[]{:S(2)}) copy-start(f32[32,72,576]{2,1,0:T(8,128)} %get-tuple-element.375) | copy-start | bytes 15925252 | tf_op jit(solution)/shard_map/while
  179.8 35.8 %copy-start.7 = (u32[32]{0:T(128)S(1)}, u32[32]{0:T(128)}, u32[]{:S(2)}) copy-start(u32[32]{0:T(128)} %constant.152) | copy-start | bytes 388
  179.8 37.8 %copy-start.4 = (bf16[36,3584]{1,0:T(8,128)(2,1)S(1)}, bf16[36,3584]{1,0:T(8,128)(2,1)}, u32[]{:S(2)}) copy-start(bf16[36,3584]{1,0:T(8,128)(2,1)} %param.19) | copy-start | bytes 774148
  179.8 38.0 %copy-start.5 = (f32[3584]{0:T(1024)S(1)}, f32[3584]{0:T(1024)}, u32[]{:S(2)}) copy-start(f32[3584]{0:T(1024)} %param.20) | copy-start | bytes 43012
  213.1 4.0 %collective-permute-start = (bf16[4,3584]{1,0:T(4,128)(2,1)S(1)}, bf16[4,3584]{1,0:T(4,128)(2,1)S(1)}, u32[]{:S(2)}, u32[]{:S(2)}) collective-permute-start(bf16[4,3584]{1,0:T(4,128)(2,1)S(1)} %slice), channel_id=1, source_target_pairs={{0,16},{1,17},{2,18},{3,19},{4,20},{5,21},{6,22},{7,23},{8,24},{9,... | collective-permute-start | bytes 86024
Sparse Core Ops, SparseCore 0:
  10.3 41.0 all-gather.3
  93.2 79.7 all-gather.5
where the time goes:
time: 226 us
  waiting for transfers between devices  94.3 us (42%)
  blocking collectives  56.1 us (25%)
  matrix products  42.8 us (19%)
  between operations  14.9 us (7%)
  other arithmetic  10.7 us (5%)
  local copies, waits for them, and re-layouts  4.29 us (2%)
  starting transfers between devices  2.54 us (1%)
    all_gather x1, waiting for transfers between devices, per_device(): every_row = lax.all_gather(heads_out, 'seq', axis=0, tiled=True)  79.9 us
    all_gather x1, blocking collectives, per_device(): lax.all_gather(key_rope, 'seq', axis=0, tiled=True)  24.1 us
    all_to_all x1, blocking collectives, per_device(): lax.all_to_all(columns, 'seq', split_axis=0, concat_axis=1, tiled=True)  20.2 us
    all_gather x1, waiting for transfers between devices, per_device(): lax.all_gather(latent, 'seq', axis=0, tiled=True)  13.4 us
    unnamed x1, blocking collectives  11.8 us
    dot_general x2, matrix products, attend(): jnp.einsum('htn,nl->htl', weight.astype(jnp.bfloat16), lat_piece, preferr...  10.4 us
    dot_general x2, matrix products, attend(): jnp.einsum('htr,nr->htn', rotary, rope_piece, preferred_element_type=jnp....  8.46 us
    reduce_sum x2, other arithmetic, attend(): total = total * factor + jnp.sum(weight, axis=2)  8.21 us
  transfers between devices with their start and end apart: 3, of which 3 were waited for; matrix products, arithmetic and copies ran while one was open for 3% of the time, Pallas kernels for 0%

commit v1 on v0

--- a/solution.py
+++ b/solution.py
@@ -89,9 +89,10 @@
     heads_out = per_head.reshape(tok_rows, local_heads * per_head.shape[2])
     every_row = lax.all_gather(heads_out, "seq", axis=0, tiled=True)
     columns = jnp.dot(every_row, w_out, preferred_element_type=jnp.float32).astype(jnp.bfloat16)
-    partial_value = lax.all_to_all(columns, "seq", split_axis=0, concat_axis=1, tiled=True).astype(
-        jnp.float32
-    )
+    partial_value = jnp.concatenate(
+        lax.all_to_all(jnp.stack(jnp.split(columns, lax.axis_size("seq"), axis=0)), "seq", 0, 0),
+        axis=1,
+    ).astype(jnp.float32)
     projected = lax.psum_scatter(
         partial_value.astype(jnp.bfloat16), "heads", scatter_dimension=0, tiled=True
     ).astype(jnp.float32)

time: 226 us -> 238 us (1.053)
  local copies, waits for them, and re-layouts: 4.29 us -> 16.7 us
    unnamed x14 -> x29, local copies, waits for them, and re-layouts: 1.33 us -> 11.8 us
where the time goes in v1:
time: 238 us
  waiting for transfers between devices  94.3 us (40%)
  blocking collectives  56.1 us (24%)
  matrix products  42.8 us (18%)
  local copies, waits for them, and re-layouts  16.7 us (7%)
  between operations  14.9 us (6%)
  other arithmetic  10.7 us (4%)
  starting transfers between devices  2.54 us (1%)
    all_gather x1, waiting for transfers between devices, per_device(): every_row = lax.all_gather(heads_out, 'seq', axis=0, tiled=True)  79.9 us
    all_gather x1, blocking collectives, per_device(): lax.all_gather(key_rope, 'seq', axis=0, tiled=True)  24.1 us
    all_to_all x1, blocking collectives, per_device(): lax.all_to_all(jnp.stack(jnp.split(columns, lax.axis_size('seq'), axis=0)...  20.2 us
    all_gather x1, waiting for transfers between devices, per_device(): lax.all_gather(latent, 'seq', axis=0, tiled=True)  13.4 us
    unnamed x29, local copies, waits for them, and re-layouts  11.8 us
    unnamed x1, blocking collectives  11.8 us
    dot_general x2, matrix products, attend(): jnp.einsum('htn,nl->htl', weight.astype(jnp.bfloat16), lat_piece, preferr...  10.4 us
    dot_general x2, matrix products, attend(): jnp.einsum('htr,nr->htn', rotary, rope_piece, preferred_element_type=jnp....  8.46 us
  transfers between devices with their start and end apart: 3, of which 3 were waited for; matrix products, arithmetic and copies ran while one was open for 3% of the time, Pallas kernels for 0%

profile of v1, /device:TPU:0, one launch (start us, length us, event | category | flops | bytes accessed | tf_op | source)
XLA Modules:
  0.0 238.1 jit_solution(13284421098275285304)
XLA Ops:
  8.0 24.1 %all-gather = bf16[16,72,64]{1,2,0:T(8,128)(2,1)S(1)} all-gather(bf16[1,72,64]{1,2,0:T(8,128)(2,1)} %bitcast.109), channel_id=1, replica_groups=mesh['heads'=2,'seq'=16] {'seq'}, dimensions={0}, use_global_device_ids=true | all-gather | bytes 156672 | tf_op jit(solution)/shard_map/all_gather | solution.py:73
  32.6 0.7 select_reduce_fusion.1
  33.4 4.7 %convolution_convert_fusion.1 = bf16[32,72,512]{2,1,0:T(8,128)(2,1)} fusion(bf16[32,128,512]{2,1,0:T(8,128)(2,1)} %param.16, bf16[72,32,128]{2,1,0:T(8,128)(2,1)} %param.12), kind=kOutput, calls=%fused_computation.41 | convolution fusion | flops 303169536 | bytes 7143424 | tf_op jit(solution)/shard_map/thd,hdl->htl/dot_general | solution.py:37
  38.0 13.4 %all-gather.4.cloned.1.call-done = bf16[1152,512]{1,0:T(8,128)(2,1)} async-done(((bf16[72,512]{1,0:T(8,128)(2,1)}), bf16[1152,512]{1,0:T(8,128)(2,1)}) %all-gather.4.cloned.1.call-update) | async-done | bytes 1179664 | tf_op jit(solution)/shard_map/all_gather | solution.py:72
  51.4 36.1 %while.20 = (s32[]{:T(128)}, f32[32,72]{1,0:T(8,128)S(1)}, f32[32,72]{1,0:T(8,128)S(1)}, f32[32,72,512]{2,1,0:T(8,128)}, s32[32]{0:T(128)S(1)}, /*index=5*/s32[7...) while((s32[]{:T(128)}, f32[32,72]{1,0:T(8,128)S(1)}, ...), condition=%wide.region_5.6_spmd.clone, body=%wide.region_1.5_spmd.clone.sunk | while | flops 2904706304 | bytes 68787400 | solution.py:84
  51.4 3.9 %fusion.75 = f32[576,32,72]{0,2,1:T(8,128)S(1)} fusion(bf16[32,72,512]{2,1,0:T(8,128)(2,1)} %get-tuple-element.413, bf16[1152,512]{1,0:T(8,128)(2,1)} %get-tuple-element.412, s32[]{:T(128)S(6)} %select_n.141), kind=kOutput, calls=%fused_computation.11.clone.1 | convolution fusion | flops 1358954496 | bytes 8257540 | tf_op jit(solution)/shard_map/while/body/eval_jaxpr/htl,nl->htn/dot_general | solution.py:47
  55.6 4.2 %fusion.77 = (f32[32,72]{1,0:T(8,128)S(1)}, f32[32,72,576]{2,1,0:T(8,128)}) fusion(f32[576,32,72]{0,2,1:T(8,128)S(1)} %fusion.75, bf16[32,72,64]{1,2,0:T(8,128)(2,1)S(1)} %copy-done.3, bf16[1152,64]{0,1:T(8,128)(2,1)S(1)} %get-tuple-element.414, s32[]{:T(128)S(6)} %select_n.141, pred[72,576]{1,0:T(8,128)(4,1)S(1)} %broadcast_compare_fusion.2), kind=kOutput, calls=%fused_computation.90.clone.1 | convolution fusion | flops 175175424 | bytes 11868164 | tf_op jit(solution)/shard_map/while/body/eval_jaxpr/htr,nr->htn/dot_general | solution.py:50
  59.9 4.1 %fusion.78 = f32[32,72]{1,0:T(8,128)S(1)} fusion(f32[32,72,576]{2,1,0:T(8,128)} %get-tuple-element.375, f32[32,72]{1,0:T(8,128)S(1)} %select_maximum_fusion.2, pred[72,576]{1,0:T(8,128)(4,1)S(1)} %broadcast_compare_fusion.2), kind=kLoop, calls=%fused_computation.3.clone.1 | loop fusion | flops 3979008 | bytes 5368320 | tf_op jit(solution)/shard_map/while/body/eval_jaxpr/reduce_sum | solution.py:57
  64.3 4.4 %fusion.80 = f32[32,72,512]{2,1,0:T(8,128)} fusion(f32[32,72,512]{2,1,0:T(8,128)} %get-tuple-element.395, f32[32,72]{1,0:T(8,128)S(1)} %get-tuple-element.377, pred[]{:T(512)S(6)} %compare.3, f32[32,72,576]{2,1,0:T(8,128)S(1)} %copy-done.1, f32[32,72]{1,0:T(8,128)S(1)} %select_maximum_fusion.2, pred[72,576]{1,0:T(8,128)(4,1)S(1)} %broadcast_compare_fusion.2, ...), kind=kOutput, calls=%fused_computation.5.clone.1 | convolution fusion | flops 1366474752 | bytes 16004101 | tf_op jit(solution)/shard_map/while/body/eval_jaxpr/htn,nl->htl/dot_general | solution.py:58
  68.6 3.9 %fusion.75 = f32[576,32,72]{0,2,1:T(8,128)S(1)} fusion(bf16[32,72,512]{2,1,0:T(8,128)(2,1)} %get-tuple-element.413, bf16[1152,512]{1,0:T(8,128)(2,1)} %get-tuple-element.412, s32[]{:T(128)S(6)} %select_n.141), kind=kOutput, calls=%fused_computation.11.clone.1 | convolution fusion | flops 1358954496 | bytes 8257540 | tf_op jit(solution)/shard_map/while/body/eval_jaxpr/htl,nl->htn/dot_general | solution.py:47
  72.8 4.2 %fusion.77 = (f32[32,72]{1,0:T(8,128)S(1)}, f32[32,72,576]{2,1,0:T(8,128)}) fusion(f32[576,32,72]{0,2,1:T(8,128)S(1)} %fusion.75, bf16[32,72,64]{1,2,0:T(8,128)(2,1)S(1)} %copy-done.3, bf16[1152,64]{0,1:T(8,128)(2,1)S(1)} %get-tuple-element.414, s32[]{:T(128)S(6)} %select_n.141, pred[72,576]{1,0:T(8,128)(4,1)S(1)} %broadcast_compare_fusion.2), kind=kOutput, calls=%fused_computation.90.clone.1 | convolution fusion | flops 175175424 | bytes 11868164 | tf_op jit(solution)/shard_map/while/body/eval_jaxpr/htr,nr->htn/dot_general | solution.py:50
  77.1 4.1 %fusion.78 = f32[32,72]{1,0:T(8,128)S(1)} fusion(f32[32,72,576]{2,1,0:T(8,128)} %get-tuple-element.375, f32[32,72]{1,0:T(8,128)S(1)} %select_maximum_fusion.2, pred[72,576]{1,0:T(8,128)(4,1)S(1)} %broadcast_compare_fusion.2), kind=kLoop, calls=%fused_computation.3.clone.1 | loop fusion | flops 3979008 | bytes 5368320 | tf_op jit(solution)/shard_map/while/body/eval_jaxpr/reduce_sum | solution.py:57
  81.5 6.0 %fusion.80 = f32[32,72,512]{2,1,0:T(8,128)} fusion(f32[32,72,512]{2,1,0:T(8,128)} %get-tuple-element.395, f32[32,72]{1,0:T(8,128)S(1)} %get-tuple-element.377, pred[]{:T(512)S(6)} %compare.3, f32[32,72,576]{2,1,0:T(8,128)S(1)} %copy-done.1, f32[32,72]{1,0:T(8,128)S(1)} %select_maximum_fusion.2, pred[72,576]{1,0:T(8,128)(4,1)S(1)} %broadcast_compare_fusion.2, ...), kind=kOutput, calls=%fused_computation.5.clone.1 | convolution fusion | flops 1366474752 | bytes 16004101 | tf_op jit(solution)/shard_map/while/body/eval_jaxpr/htn,nl->htl/dot_general | solution.py:58
  87.5 4.6 %fusion.31 = bf16[32,9,8,128]{3,2,1,0:T(8,128)(2,1)S(1)} fusion(bf16[32,512,128]{2,1,0:T(8,128)(2,1)} %param.17, f32[32,72,512]{2,1,0:T(8,128)} %get-tuple-element.248, f32[32,72]{1,0:T(8,128)S(1)} %get-tuple-element.249), kind=kOutput, calls=%fused_computation.43 | convolution fusion | flops 304644096 | bytes 9511936 | tf_op jit(solution)/shard_map/htl,hle->the/dot_general | solution.py:86
  92.1 0.9 copy.36
  93.1 79.9 %all-gather.6.cloned.1.call-done = bf16[1152,4096]{1,0:T(8,128)(2,1)} async-done(((bf16[72,4096]{1,0:T(8,128)(2,1)}), bf16[1152,4096]{1,0:T(8,128)(2,1)}) %all-gather.6.cloned.1.call-update) | async-done | bytes 9437200 | tf_op jit(solution)/shard_map/all_gather | solution.py:90
  173.0 6.7 %convolution_convert_fusion = bf16[1152,224]{0,1:T(8,128)(2,1)S(1)} fusion(bf16[1152,4096]{1,0:T(8,128)(2,1)} %all-gather.6.cloned.1.call-done, bf16[4096,224]{0,1:T(8,128)(2,1)S(1)} %copy-done), kind=kOutput, calls=%fused_computation.39 | convolution fusion | flops 2114187264 | bytes 11788288 | tf_op jit(solution)/shard_map/dot_general | solution.py:91
  186.0 0.7 fusion.40
  191.0 1.5 copy.30
  192.5 20.2 %all_to_all.5 = bf16[16,72,224]{2,1,0:T(8,128)(2,1)S(1)} all-to-all(bf16[16,72,224]{2,1,0:T(8,128)(2,1)S(1)} %copy.30), channel_id=1, replica_groups=mesh['heads'=2,'seq'=16] {'seq'}, dimensions={0} | all-to-all | bytes 1032192 | tf_op jit(solution)/shard_map/all_to_all | solution.py:93
  212.8 1.0 reshape.99
  213.7 11.8 %fusion = bf16[40,3584]{1,0:T(8,128)(2,1)S(1)} fusion(bf16[72,3584]{1,0:T(8,128)(2,1)S(1)} %reshape.99), kind=kCustom, calls=%all-reduce-scatter | all-reduce-scatter fusion | flops 286721 | bytes 803328
  225.6 2.5 %collective-permute-start = (bf16[4,3584]{1,0:T(4,128)(2,1)S(1)}, bf16[4,3584]{1,0:T(4,128)(2,1)S(1)}, u32[]{:S(2)}, u32[]{:S(2)}) collective-permute-start(bf16[4,3584]{1,0:T(4,128)(2,1)S(1)} %slice), channel_id=1, source_target_pairs={{0,16},{1,17},{2,18},{3,19},{4,20},{5,21},{6,22},{7,23},{8,24},{9,... | collective-permute-start | bytes 86024
  230.3 1.0 multiply_convert_fusion
  (69 shorter events, 14.5 us)
Async XLA Ops:
  7.2 165.8 %copy-start = (bf16[4096,224]{0,1:T(8,128)(2,1)S(1)}, bf16[4096,224]{0,1:T(8,128)(2,1)}, u32[]{:S(2)}) copy-start(bf16[4096,224]{0,1:T(8,128)(2,1)} %param.18) | copy-start | bytes 5505028
  7.2 44.2 %copy-start.6 = (s32[32]{0:T(128)S(1)}, s32[32]{0:T(128)}, u32[]{:S(2)}) copy-start(s32[32]{0:T(128)} %param.21) | copy-start | bytes 388
  7.2 44.2 %all-gather.4.cloned.1.call-start = ((), (), s32[]{:S(2)}) async-start(), calls=%async_computation.1 | async-start | bytes 1253376 | tf_op jit(solution)/shard_map/all_gather | solution.py:72
  7.9 165.1 %all-gather.6.cloned.1.call-start = ((), (), s32[]{:S(2)}) async-start(), calls=%async_computation.2 | async-start | bytes 10027008 | tf_op jit(solution)/shard_map/all_gather | solution.py:90
  51.4 4.2 %copy-start.3 = (bf16[32,72,64]{1,2,0:T(8,128)(2,1)S(1)}, bf16[32,72,64]{1,2,0:T(8,128)(2,1)}, u32[]{:S(2)}) copy-start(bf16[32,72,64]{1,2,0:T(8,128)(2,1)} %get-tuple-element.415) | copy-start | bytes 884740 | tf_op jit(solution)/shard_map/while
  55.6 8.4 %copy-start.2 = (bf16[1152,512]{1,0:T(8,128)(2,1)S(1)}, bf16[1152,512]{1,0:T(8,128)(2,1)}, u32[]{:S(2)}) copy-start(bf16[1152,512]{1,0:T(8,128)(2,1)} %get-tuple-element.412) | copy-start | bytes 3538948 | tf_op jit(solution)/shard_map/while
  59.8 4.4 %copy-start.1 = (f32[32,72,576]{2,1,0:T(8,128)S(1)}, f32[32,72,576]{2,1,0:T(8,128)}, u32[]{:S(2)}) copy-start(f32[32,72,576]{2,1,0:T(8,128)} %get-tuple-element.375) | copy-start | bytes 15925252 | tf_op jit(solution)/shard_map/while
  68.6 4.2 %copy-start.3 = (bf16[32,72,64]{1,2,0:T(8,128)(2,1)S(1)}, bf16[32,72,64]{1,2,0:T(8,128)(2,1)}, u32[]{:S(2)}) copy-start(bf16[32,72,64]{1,2,0:T(8,128)(2,1)} %get-tuple-element.415) | copy-start | bytes 884740 | tf_op jit(solution)/shard_map/while
  72.8 8.4 %copy-start.2 = (bf16[1152,512]{1,0:T(8,128)(2,1)S(1)}, bf16[1152,512]{1,0:T(8,128)(2,1)}, u32[]{:S(2)}) copy-start(bf16[1152,512]{1,0:T(8,128)(2,1)} %get-tuple-element.412) | copy-start | bytes 3538948 | tf_op jit(solution)/shard_map/while
  77.1 4.4 %copy-start.1 = (f32[32,72,576]{2,1,0:T(8,128)S(1)}, f32[32,72,576]{2,1,0:T(8,128)}, u32[]{:S(2)}) copy-start(f32[32,72,576]{2,1,0:T(8,128)} %get-tuple-element.375) | copy-start | bytes 15925252 | tf_op jit(solution)/shard_map/while
  179.8 48.3 %copy-start.7 = (u32[32]{0:T(128)S(1)}, u32[32]{0:T(128)}, u32[]{:S(2)}) copy-start(u32[32]{0:T(128)} %constant.152) | copy-start | bytes 388
  179.8 50.2 %copy-start.4 = (bf16[36,3584]{1,0:T(8,128)(2,1)S(1)}, bf16[36,3584]{1,0:T(8,128)(2,1)}, u32[]{:S(2)}) copy-start(bf16[36,3584]{1,0:T(8,128)(2,1)} %param.19) | copy-start | bytes 774148
  179.8 50.5 %copy-start.5 = (f32[3584]{0:T(1024)S(1)}, f32[3584]{0:T(1024)}, u32[]{:S(2)}) copy-start(f32[3584]{0:T(1024)} %param.20) | copy-start | bytes 43012
  225.6 4.0 %collective-permute-start = (bf16[4,3584]{1,0:T(4,128)(2,1)S(1)}, bf16[4,3584]{1,0:T(4,128)(2,1)S(1)}, u32[]{:S(2)}, u32[]{:S(2)}) collective-permute-start(bf16[4,3584]{1,0:T(4,128)(2,1)S(1)} %slice), channel_id=1, source_target_pairs={{0,16},{1,17},{2,18},{3,19},{4,20},{5,21},{6,22},{7,23},{8,24},{9,... | collective-permute-start | bytes 86024
Sparse Core Ops, SparseCore 0:
  10.3 41.0 all-gather.3
  93.2 79.7 all-gather.5
